TPU v7x, 256 devices: a whole 4x4x8 slice. The times are simulated.
256 devices in a mesh: blk: 4 (over z_lo), pts: 64 (over y, z_hi, x, core).
Axes of the slice: x: 4, y: 4, z: 8 (z_hi: 2, z_lo: 4; z = z_hi * 4 + z_lo), core: 2. Of those that a mesh axis runs over, the one named last changes fastest.
Arguments:
- signal: bfloat16 [67584, 16384], P('blk', 'pts'), may hold values from -6 to 6
- offsets: int32 [128], P('blk'), may hold values from 0 to 15872
- kept: int32 [128], replicated, may hold values from 0 to 512
- weights: float32 [16384], P('pts'), may hold values from 0.2 to 5
Outputs:
- gram: float32 [128, 2, 128, 128], P('pts', None, 'blk')
Inputs may be any that keep to these rules, and one draw needn't show every extreme that they name: `kept`: indices may repeat.
All inputs are finite; a program needn't handle non-finite values.
Results may differ from a plain program's by a relative error of at most 0.0022.
Values may be sent and summed in bfloat16 or wider, within the bound.
A program may use at most 128 MiB of HBM per device.

v0:
```python
import math
import jax
import jax.numpy as jnp
from jax import lax
from jax.sharding import PartitionSpec as P

NFFT = 1024


def spectral_table(kept, length):
    times = jnp.arange(length, dtype=jnp.int32)
    window = 0.5 - 0.5 * jnp.cos(times.astype(jnp.float32) * (2.0 * math.pi / length))
    norm = 1.0 / jnp.sqrt(jnp.sum(window * window))
    phase_index = times[:, None] * kept[None, :] % length
    phase = phase_index.astype(jnp.float32) * (2.0 * math.pi / length)
    cosine = (norm * window)[:, None] * jnp.cos(phase)
    sine = -(norm * window)[:, None] * jnp.sin(phase)
    return jnp.concatenate([cosine, sine], axis=1).astype(jnp.bfloat16)


def gram_terms(owned, piece):
    own_re = owned[:, 0]
    own_im = owned[:, 1]
    far_re = piece[:, 0]
    far_im = piece[:, 1]
    gram_re = jnp.einsum("bfp,nfp->fbn", own_re, far_re, preferred_element_type=jnp.float32)
    gram_re = gram_re + jnp.einsum(
        "bfp,nfp->fbn", own_im, far_im, preferred_element_type=jnp.float32
    )
    gram_im = jnp.einsum("bfp,nfp->fbn", own_re, far_im, preferred_element_type=jnp.float32)
    gram_im = gram_im - jnp.einsum(
        "bfp,nfp->fbn", own_im, far_re, preferred_element_type=jnp.float32
    )
    return jnp.stack([gram_re, gram_im], axis=1)


def on_device(signal, offsets, kept, weights):
    blocks_here = offsets.shape[0]
    points_here = signal.shape[1]
    freq_all = kept.shape[0]
    total_points = points_here * lax.axis_size("pts")
    table = spectral_table(kept, NFFT)

    def take_block(start):
        return lax.dynamic_slice(signal, (start, jnp.int32(0)), (NFFT, points_here))

    stacked = jax.vmap(take_block)(offsets)
    values = jnp.einsum("tk,btp->bkp", table, stacked, preferred_element_type=jnp.float32)
    scale = jnp.sqrt(weights / total_points)
    spectra = (
        (values * scale[None, None, :])
        .astype(jnp.bfloat16)
        .reshape(blocks_here, 2, freq_all, points_here)
    )
    moved = lax.all_to_all(spectra, "pts", split_axis=2, concat_axis=3, tiled=True)
    return gram_terms(moved, lax.all_gather(moved, "blk", axis=0, tiled=True))


def solution(mesh):
    placed = (P("blk", "pts"), P("blk"), P(), P("pts"))
    return jax.shard_map(
        on_device,
        mesh=mesh,
        in_specs=placed,
        out_specs=P("pts", None, "blk", None),
        check_vma=False,
    )
```

profile of v0, /device:TPU:1, one launch (start us, length us, event | category | flops | bytes accessed | tf_op | source)
XLA Modules:
  0.0 571.0 jit_solution(12233491624750584674)
XLA Ops:
  6.5 0.7 multiply_reduce_fusion
  7.3 0.7 multiply_sqrt_fusion
  7.9 0.7 fusion.18
  8.6 99.7 %while.1 = (s32[]{:T(128)}, bf16[16896,256]{1,0:T(8,128)(2,1)}, s32[32,2]{0,1:T(2,128)S(1)}, bf16[32,1024,256]{2,1,0:T(8,128)(2,1)}, s32[]{:T(128)}) while((s32[]{:T(128)}, bf16[16896,256]{1,0:T(8,128)(2,1)}, s32[32,2]{0,1:T(2,128)S(1)}, bf16[32,1024,256]{2,1,0:T(8,128)(2,1)}, s32[]{:T(128)}) %tuple.18), condition=%wide.while_cond, body=%wide.while_body.sunk | while | flops 2 | bytes 1049189 | solution.py:45
  8.7 0.5 slice.60
  9.2 2.5 bitcast_dynamic-update-slice_fusion.2
  12.3 2.5 bitcast_dynamic-update-slice_fusion.2
  15.4 2.5 bitcast_dynamic-update-slice_fusion.2
  18.0 0.5 slice.60
  18.5 2.5 bitcast_dynamic-update-slice_fusion.2
  21.1 0.5 slice.60
  21.6 2.5 bitcast_dynamic-update-slice_fusion.2
  24.2 0.5 slice.60
  24.7 2.5 bitcast_dynamic-update-slice_fusion.2
  27.4 0.5 slice.60
  27.9 2.5 bitcast_dynamic-update-slice_fusion.2
  30.5 0.5 slice.60
  31.0 2.5 bitcast_dynamic-update-slice_fusion.2
  33.6 0.5 slice.60
  34.1 2.5 bitcast_dynamic-update-slice_fusion.2
  37.2 2.5 bitcast_dynamic-update-slice_fusion.2
  39.8 0.5 slice.60
  40.3 2.5 bitcast_dynamic-update-slice_fusion.2
  43.5 2.5 bitcast_dynamic-update-slice_fusion.2
  46.1 0.5 slice.60
  46.6 2.5 bitcast_dynamic-update-slice_fusion.2
  49.2 0.5 slice.60
  49.7 2.5 bitcast_dynamic-update-slice_fusion.2
  52.3 0.5 slice.60
  52.8 2.5 bitcast_dynamic-update-slice_fusion.2
  55.4 0.5 slice.60
  55.9 2.6 bitcast_dynamic-update-slice_fusion.2
  59.1 2.6 bitcast_dynamic-update-slice_fusion.2
  61.7 0.5 slice.60
  62.2 2.6 bitcast_dynamic-update-slice_fusion.2
  64.8 0.5 slice.60
  65.3 2.5 bitcast_dynamic-update-slice_fusion.2
  67.9 0.5 slice.60
  68.4 2.5 bitcast_dynamic-update-slice_fusion.2
  71.5 2.6 bitcast_dynamic-update-slice_fusion.2
  74.2 0.5 slice.60
  74.7 2.5 bitcast_dynamic-update-slice_fusion.2
  77.8 2.5 bitcast_dynamic-update-slice_fusion.2
  80.9 2.5 bitcast_dynamic-update-slice_fusion.2
  84.0 2.6 bitcast_dynamic-update-slice_fusion.2
  87.1 2.5 bitcast_dynamic-update-slice_fusion.2
  90.3 2.5 bitcast_dynamic-update-slice_fusion.2
  93.4 2.5 bitcast_dynamic-update-slice_fusion.2
  96.5 2.5 bitcast_dynamic-update-slice_fusion.2
  99.6 2.5 bitcast_dynamic-update-slice_fusion.2
  102.7 2.5 bitcast_dynamic-update-slice_fusion.2
  105.8 2.5 bitcast_dynamic-update-slice_fusion.2
  109.1 3.1 multiply_convert_fusion.2
  112.3 12.1 %multiply_convert_fusion = bf16[32,256,256]{1,2,0:T(8,128)(2,1)} fusion(f32[256]{0:T(256)S(1)} %multiply_sqrt_fusion, bf16[32,1024,256]{2,1,0:T(8,128)(2,1)} %get-tuple-element.12, bf16[1024,128]{0,1:T(8,128)(2,1)S(1)} %get-tuple-element.22, bf16[1024,128]{0,1:T(8,128)(2,1)S(1)} %get-tuple-element.21), kind=kOutput, calls=%fused_computation.4 | convolution fusion | flops 4300210176 | bytes 21496832 | tf_op jit(solution)/shard_map/tk,btp->bkp/dot_general | solution.py:48
  124.4 6.5 %copy.7 = bf16[32,2,128,256]{3,1,0,2:T(2,128)(2,1)S(1)} copy(bf16[32,2,128,256]{3,2,1,0:T(8,128)(2,1)} %bitcast.62) | data formatting | bytes 8388608 | tf_op jit(solution)/shard_map/reshape | solution.py:53
  130.9 115.3 %all_to_all.18 = bf16[32,2,128,256]{3,1,0,2:T(2,128)(2,1)S(1)} all-to-all(bf16[32,2,128,256]{3,1,0,2:T(2,128)(2,1)S(1)} %copy.7), channel_id=1, replica_groups=mesh['blk'=4,'pts'=64] {'pts'}, dimensions={2} | all-to-all | bytes 8388608 | tf_op jit(solution)/shard_map/all_to_all | solution.py:55
  246.2 4.4 copy.11
  250.5 7.4 %all_to_all.16 = bf16[32,2,2,16384]{3,0,2,1:T(8,128)(2,1)} reshape(bf16[32,2,2,64,256]{4,3,0,2,1:T(8,128)(2,1)} %bitcast.61) | data formatting | bytes 8388608 | tf_op jit(solution)/shard_map/all_to_all | solution.py:55
  257.9 285.5 %all-gather.2.cloned.1.call-done = bf16[128,2,2,16384]{3,0,2,1:T(8,128)(2,1)} async-done(((bf16[32,2,2,16384]{3,0,2,1:T(8,128)(2,1)}), bf16[128,2,2,16384]{3,0,2,1:T(8,128)(2,1)}) %all-gather.2.cloned.1.call-update) | async-done | bytes 16777232 | tf_op jit(solution)/shard_map/all_gather | solution.py:56
  543.4 7.1 %fusion = f32[2,32,128]{2,1,0:T(8,128)S(1)} fusion(bf16[128,2,2,16384]{3,0,2,1:T(8,128)(2,1)} %all-gather.2.cloned.1.call-done, bf16[32,2,2,16384]{3,0,2,1:T(8,128)(2,1)} %all_to_all.16), kind=kOutput, calls=%fused_computation.5 | convolution fusion | flops 268435456 | bytes 10518528 | tf_op jit(solution)/shard_map/bfp,nfp->fbn/dot_general | solution.py:31
  550.5 7.0 %fusion.1 = f32[2,32,128]{2,1,0:T(8,128)S(1)} fusion(bf16[128,2,2,16384]{3,0,2,1:T(8,128)(2,1)} %all-gather.2.cloned.1.call-done, bf16[32,2,2,16384]{3,0,2,1:T(8,128)(2,1)S(1)} %copy-done), kind=kOutput, calls=%fused_computation.6 | convolution fusion | flops 268435456 | bytes 10518528 | tf_op jit(solution)/shard_map/bfp,nfp->fbn/dot_general | solution.py:26
  557.6 2.9 fusion.7
  560.5 3.0 fusion.5
  563.5 0.6 copy.9
  (58 shorter events, 10.6 us)
Async XLA Ops:
  6.5 536.9 %all-gather.2.cloned.1.call-start = ((), (), s32[]{:S(2)}) async-start(), calls=%async_computation.1 | async-start | bytes 20971520 | tf_op jit(solution)/shard_map/all_gather | solution.py:56
  543.4 7.1 %copy-start = (bf16[32,2,2,16384]{3,0,2,1:T(8,128)(2,1)S(1)}, bf16[32,2,2,16384]{3,0,2,1:T(8,128)(2,1)}, u32[]{:S(2)}) copy-start(bf16[32,2,2,16384]{3,0,2,1:T(8,128)(2,1)} %all_to_all.16) | copy-start | bytes 12582916
  543.4 14.1 %copy-start.1 = (bf16[128,2,2,16384]{3,0,2,1:T(8,128)(2,1)S(1)}, bf16[128,2,2,16384]{3,0,2,1:T(8,128)(2,1)}, u32[]{:S(2)}) copy-start(bf16[128,2,2,16384]{3,0,2,1:T(8,128)(2,1)} %all-gather.2.cloned.1.call-done) | copy-start | bytes 50331652
Sparse Core Ops, SparseCore 0:
  258.1 285.3 all-gather.1
where the time goes:
time: 573 us; the launch traced here: 571 us
  waiting for transfers between devices  286 us (50%)
  local copies, waits for them, and re-layouts  119 us (21%)
  blocking collectives  115 us (20%)
  matrix products  32 us (6%)
  between operations  14.2 us (2%)
    all_gather x1, waiting for transfers between devices, on_device(): return gram_terms(moved, lax.all_gather(moved, 'blk', axis=0, tiled=True))  285 us
    all_to_all x1, blocking collectives, on_device(): lax.all_to_all(spectra, 'pts', split_axis=2, concat_axis=3, tiled=True)  115 us
    gather x96, local copies, waits for them, and re-layouts  99.7 us
    dot_general x1, matrix products, on_device(): jnp.einsum('tk,btp->bkp', table, stacked, preferred_element_type=jnp.floa...  12.1 us
    all_to_all x2, local copies, waits for them, and re-layouts, on_device(): lax.all_to_all(spectra, 'pts', split_axis=2, concat_axis=3, tiled=True)  11.8 us
  transfers between devices with their start and end apart: 1, of which 1 were waited for; matrix products, arithmetic and copies ran while one was open for 0% of the time, Pallas kernels for 0%

commit v1 on v0

--- a/solution.py
+++ b/solution.py
@@ -53,7 +53,12 @@
         .reshape(blocks_here, 2, freq_all, points_here)
     )
     moved = lax.all_to_all(spectra, "pts", split_axis=2, concat_axis=3, tiled=True)
-    return gram_terms(moved, lax.all_gather(moved, "blk", axis=0, tiled=True))
+    return gram_terms(
+        moved,
+        jnp.concatenate(
+            lax.all_to_all(jnp.stack([moved] * lax.axis_size("blk")), "blk", 0, 0), axis=0
+        ),
+    )
 
 
 def solution(mesh):

time: 573 us -> 654 us (1.14)
  blocking collectives: 115 us -> 481 us
  waiting for transfers between devices: 286 us -> 0 us
  local copies, waits for them, and re-layouts: 119 us -> 133 us
  between operations: 14.2 us -> 0.75 us
    all_to_all x0 -> x1, blocking collectives: none -> 366 us  [on_device(): lax.all_to_all(jnp.stack([moved] * lax.axis_size('blk')), 'blk', 0, 0)]
    all_gather x1 -> x0, waiting for transfers between devices: 285 us -> none  [on_device(): return gram_terms(moved, lax.all_gather(moved, 'blk', axis=0, tiled=True))]
    all_to_all x0 -> x1, local copies, waits for them, and re-layouts: none -> 7.05 us  [on_device(): lax.all_to_all(jnp.stack([moved] * lax.axis_size('blk')), 'blk', 0, 0)]
  transfers between devices with their start and end apart: 1 -> 0, of which waited for: 1 -> 0; matrix products, arithmetic and copies ran while one was open for 0% -> 0% of each run, Pallas kernels for 0% -> 0%
where the time goes in v1:
time: 654 us; the launch traced here: 652 us
  blocking collectives  481 us (74%)
  local copies, waits for them, and re-layouts  133 us (20%)
  matrix products  31.4 us (5%)
    all_to_all x1, blocking collectives, on_device(): lax.all_to_all(jnp.stack([moved] * lax.axis_size('blk')), 'blk', 0, 0)  366 us
    all_to_all x1, blocking collectives, on_device(): lax.all_to_all(spectra, 'pts', split_axis=2, concat_axis=3, tiled=True)  115 us
    gather x96, local copies, waits for them, and re-layouts  103 us

profile of v1, /device:TPU:1, one launch (start us, length us, event | category | flops | bytes accessed | tf_op | source)
XLA Modules:
  0.0 651.8 jit_solution(15144942700518701893)
XLA Ops:
  0.0 0.6 multiply_reduce_fusion
  1.3 0.7 fusion.18
  2.0 0.7 multiply_sqrt_fusion
  2.8 103.3 %while.1 = (s32[]{:T(128)}, bf16[16896,256]{1,0:T(8,128)(2,1)}, s32[32,2]{0,1:T(2,128)S(1)}, bf16[32,1024,256]{2,1,0:T(8,128)(2,1)}, s32[]{:T(128)}) while((s32[]{:T(128)}, bf16[16896,256]{1,0:T(8,128)(2,1)}, s32[32,2]{0,1:T(2,128)S(1)}, bf16[32,1024,256]{2,1,0:T(8,128)(2,1)}, s32[]{:T(128)}) %tuple.18), condition=%wide.while_cond, body=%wide.while_body.sunk | while | flops 2 | bytes 1049189 | solution.py:45
  2.8 0.5 slice.60
  3.4 2.6 bitcast_dynamic-update-slice_fusion.2
  6.1 0.5 slice.60
  6.6 2.6 bitcast_dynamic-update-slice_fusion.2
  9.3 0.5 slice.60
  9.8 2.6 bitcast_dynamic-update-slice_fusion.2
  13.0 2.6 bitcast_dynamic-update-slice_fusion.2
  15.7 0.5 slice.60
  16.2 2.6 bitcast_dynamic-update-slice_fusion.2
  18.9 0.5 slice.60
  19.5 2.6 bitcast_dynamic-update-slice_fusion.2
  22.7 2.6 bitcast_dynamic-update-slice_fusion.2
  25.4 0.5 slice.60
  25.9 2.6 bitcast_dynamic-update-slice_fusion.2
  28.6 0.5 slice.60
  29.1 2.6 bitcast_dynamic-update-slice_fusion.2
  32.3 2.6 bitcast_dynamic-update-slice_fusion.2
  35.0 0.5 slice.60
  35.6 2.6 bitcast_dynamic-update-slice_fusion.2
  38.3 0.5 slice.60
  38.8 2.6 bitcast_dynamic-update-slice_fusion.2
  41.5 0.5 slice.60
  42.0 2.6 bitcast_dynamic-update-slice_fusion.2
  45.3 2.6 bitcast_dynamic-update-slice_fusion.2
  48.5 2.6 bitcast_dynamic-update-slice_fusion.2
  51.2 0.5 slice.60
  51.7 2.6 bitcast_dynamic-update-slice_fusion.2
  54.9 2.7 bitcast_dynamic-update-slice_fusion.2
  58.2 2.7 bitcast_dynamic-update-slice_fusion.2
  60.9 0.5 slice.60
  61.5 2.6 bitcast_dynamic-update-slice_fusion.2
  64.7 2.6 bitcast_dynamic-update-slice_fusion.2
  67.4 0.5 slice.60
  67.9 2.6 bitcast_dynamic-update-slice_fusion.2
  70.6 0.5 slice.60
  71.1 2.6 bitcast_dynamic-update-slice_fusion.2
  74.4 2.6 bitcast_dynamic-update-slice_fusion.2
  77.6 2.6 bitcast_dynamic-update-slice_fusion.2
  80.8 2.6 bitcast_dynamic-update-slice_fusion.2
  84.0 2.6 bitcast_dynamic-update-slice_fusion.2
  87.3 2.6 bitcast_dynamic-update-slice_fusion.2
  90.5 2.6 bitcast_dynamic-update-slice_fusion.2
  93.7 2.6 bitcast_dynamic-update-slice_fusion.2
  96.9 2.6 bitcast_dynamic-update-slice_fusion.2
  100.2 2.6 bitcast_dynamic-update-slice_fusion.2
  103.4 2.6 bitcast_dynamic-update-slice_fusion.2
  106.0 3.1 multiply_convert_fusion.2
  109.2 12.1 %multiply_convert_fusion = bf16[32,256,256]{1,2,0:T(8,128)(2,1)} fusion(f32[256]{0:T(256)S(1)} %multiply_sqrt_fusion, bf16[32,1024,256]{2,1,0:T(8,128)(2,1)} %get-tuple-element.12, bf16[1024,128]{0,1:T(8,128)(2,1)S(1)} %get-tuple-element.22, bf16[1024,128]{0,1:T(8,128)(2,1)S(1)} %get-tuple-element.21), kind=kOutput, calls=%fused_computation.4 | convolution fusion | flops 4300210176 | bytes 21496832 | tf_op jit(solution)/shard_map/tk,btp->bkp/dot_general | solution.py:48
  121.2 6.5 copy.7
  127.7 115.3 %all_to_all.23 = bf16[32,2,128,256]{3,1,0,2:T(2,128)(2,1)S(1)} all-to-all(bf16[32,2,128,256]{3,1,0,2:T(2,128)(2,1)S(1)} %copy.7), channel_id=1, replica_groups=mesh['blk'=4,'pts'=64] {'pts'}, dimensions={2} | all-to-all | bytes 8388608 | tf_op jit(solution)/shard_map/all_to_all | solution.py:55
  243.1 4.4 copy.12
  247.4 7.4 %all_to_all.19 = bf16[32,2,2,16384]{3,0,2,1:T(8,128)(2,1)} reshape(bf16[32,2,2,64,256]{4,3,0,2,1:T(8,128)(2,1)} %bitcast.66) | data formatting | bytes 8388608 | tf_op jit(solution)/shard_map/all_to_all | solution.py:55
  254.8 3.9 stack.16
  258.7 366.0 %all_to_all.24 = bf16[4,32,2,2,16384]{4,1,3,2,0:T(8,128)(2,1)S(1)} all-to-all(bf16[4,32,2,2,16384]{4,1,3,2,0:T(8,128)(2,1)S(1)} %stack.16), channel_id=1, replica_groups=mesh['blk'=4,'pts'=64] {'blk'}, dimensions={0} | all-to-all | bytes 33554432 | tf_op jit(solution)/shard_map/all_to_all | solution.py:59
  624.7 7.0 %copy.9 = bf16[4,32,2,2,16384]{4,1,0,3,2:T(8,128)(2,1)} copy(bf16[4,32,2,2,16384]{4,1,3,2,0:T(8,128)(2,1)S(1)} %all_to_all.24) | data formatting | bytes 33554432 | tf_op jit(solution)/shard_map/all_to_all | solution.py:59
  631.8 6.4 fusion
  638.2 7.0 %fusion.1 = f32[2,32,128]{2,1,0:T(8,128)S(1)} fusion(bf16[128,2,2,16384]{3,0,2,1:T(8,128)(2,1)} %bitcast.62, bf16[32,2,2,16384]{3,0,2,1:T(8,128)(2,1)S(1)} %copy-done), kind=kOutput, calls=%fused_computation.6 | convolution fusion | flops 268435456 | bytes 10518528 | tf_op jit(solution)/shard_map/bfp,nfp->fbn/dot_general | solution.py:26
  645.2 2.9 fusion.7
  648.1 3.0 fusion.5
  651.1 0.6 copy.10
  (58 shorter events, 12.1 us)
Async XLA Ops:
  624.7 7.1 %copy-start = (bf16[32,2,2,16384]{3,0,2,1:T(8,128)(2,1)S(1)}, bf16[32,2,2,16384]{3,0,2,1:T(8,128)(2,1)}, u32[]{:S(2)}) copy-start(bf16[32,2,2,16384]{3,0,2,1:T(8,128)(2,1)} %all_to_all.19) | copy-start | bytes 12582916
  631.8 13.4 %copy-start.1 = (bf16[4,32,2,2,16384]{4,1,0,3,2:T(8,128)(2,1)S(1)}, bf16[4,32,2,2,16384]{4,1,0,3,2:T(8,128)(2,1)}, u32[]{:S(2)}) copy-start(bf16[4,32,2,2,16384]{4,1,0,3,2:T(8,128)(2,1)} %copy.9) | copy-start | bytes 50331652

commit v2 on v0

--- a/solution.py
+++ b/solution.py
@@ -52,7 +52,10 @@
         .astype(jnp.bfloat16)
         .reshape(blocks_here, 2, freq_all, points_here)
     )
-    moved = lax.all_to_all(spectra, "pts", split_axis=2, concat_axis=3, tiled=True)
+    moved = jnp.concatenate(
+        lax.all_to_all(jnp.stack(jnp.split(spectra, lax.axis_size("pts"), axis=2)), "pts", 0, 0),
+        axis=3,
+    )
     return gram_terms(moved, lax.all_gather(moved, "blk", axis=0, tiled=True))
 
 

time: 573 us -> 576 us (level)
    all_to_all x2 -> x0, local copies, waits for them, and re-layouts: 11.8 us -> none  [on_device(): lax.all_to_all(spectra, 'pts', split_axis=2, concat_axis=3, tiled=True)]
    gather x96, local copies, waits for them, and re-layouts: 99.7 us -> 106 us
    reshape x1 -> x2, local copies, waits for them, and re-layouts: 6.5 us -> 11.7 us  [on_device(): jnp.concatenate(lax.all_to_all(jnp.stack(jnp.split(spectra, lax.axis_size...]
where the time goes in v2:
time: 576 us; the launch traced here: 574 us
  waiting for transfers between devices  286 us (50%)
  local copies, waits for them, and re-layouts  124 us (22%)
  blocking collectives  115 us (20%)
  matrix products  30.7 us (5%)
  between operations  14.2 us (2%)
    all_gather x1, waiting for transfers between devices, on_device(): return gram_terms(moved, lax.all_gather(moved, 'blk', axis=0, tiled=True))  285 us
    all_to_all x1, blocking collectives, on_device(): lax.all_to_all(jnp.stack(jnp.split(spectra, lax.axis_size('pts'), axis=2)...  115 us
    gather x96, local copies, waits for them, and re-layouts  106 us
    reshape x2, local copies, waits for them, and re-layouts, on_device(): jnp.concatenate(lax.all_to_all(jnp.stack(jnp.split(spectra, lax.axis_size...  11.7 us
  transfers between devices with their start and end apart: 1, of which 1 were waited for; matrix products, arithmetic and copies ran while one was open for 0% of the time, Pallas kernels for 0%

profile of v2, /device:TPU:1, one launch (start us, length us, event | category | flops | bytes accessed | tf_op | source)
XLA Modules:
  0.0 574.2 jit_solution(8861612060647347051)
XLA Ops:
  6.5 0.6 multiply_reduce_fusion
  7.2 0.7 multiply_sqrt_fusion
  7.9 0.7 fusion.18
  8.5 106.5 %while.1 = (s32[]{:T(128)}, bf16[16896,256]{1,0:T(8,128)(2,1)}, s32[32,2]{0,1:T(2,128)S(1)}, bf16[32,1024,256]{2,1,0:T(8,128)(2,1)}, s32[]{:T(128)}) while((s32[]{:T(128)}, bf16[16896,256]{1,0:T(8,128)(2,1)}, s32[32,2]{0,1:T(2,128)S(1)}, bf16[32,1024,256]{2,1,0:T(8,128)(2,1)}, s32[]{:T(128)}) %tuple.18), condition=%wide.while_cond, body=%wide.while_body.sunk | while | flops 2 | bytes 1049189 | solution.py:45
  8.6 0.6 slice.60
  9.2 2.7 bitcast_dynamic-update-slice_fusion.2
  11.9 0.6 slice.60
  12.5 2.7 bitcast_dynamic-update-slice_fusion.2
  15.3 0.6 slice.60
  15.8 2.7 bitcast_dynamic-update-slice_fusion.2
  18.6 0.6 slice.60
  19.2 2.7 bitcast_dynamic-update-slice_fusion.2
  21.9 0.6 slice.60
  22.5 2.7 bitcast_dynamic-update-slice_fusion.2
  25.2 0.6 slice.60
  25.8 2.7 bitcast_dynamic-update-slice_fusion.2
  28.6 0.6 slice.60
  29.2 2.7 bitcast_dynamic-update-slice_fusion.2
  31.9 0.6 slice.60
  32.5 2.7 bitcast_dynamic-update-slice_fusion.2
  35.2 0.6 slice.60
  35.8 2.7 bitcast_dynamic-update-slice_fusion.2
  38.5 0.6 slice.60
  39.1 2.7 bitcast_dynamic-update-slice_fusion.2
  41.9 0.6 slice.60
  42.4 2.7 bitcast_dynamic-update-slice_fusion.2
  45.2 0.6 slice.60
  45.8 2.7 bitcast_dynamic-update-slice_fusion.2
  48.5 0.6 slice.60
  49.1 2.7 bitcast_dynamic-update-slice_fusion.2
  51.8 0.6 slice.60
  52.4 2.7 bitcast_dynamic-update-slice_fusion.2
  55.2 0.6 slice.60
  55.8 2.6 bitcast_dynamic-update-slice_fusion.2
  58.5 0.6 slice.60
  59.1 2.7 bitcast_dynamic-update-slice_fusion.2
  61.9 0.6 slice.60
  62.4 2.7 bitcast_dynamic-update-slice_fusion.2
  65.8 2.7 bitcast_dynamic-update-slice_fusion.2
  69.2 2.7 bitcast_dynamic-update-slice_fusion.2
  72.5 2.6 bitcast_dynamic-update-slice_fusion.2
  75.8 2.7 bitcast_dynamic-update-slice_fusion.2
  79.1 2.7 bitcast_dynamic-update-slice_fusion.2
  82.5 2.6 bitcast_dynamic-update-slice_fusion.2
  85.8 2.7 bitcast_dynamic-update-slice_fusion.2
  89.1 2.7 bitcast_dynamic-update-slice_fusion.2
  92.4 2.7 bitcast_dynamic-update-slice_fusion.2
  95.8 2.7 bitcast_dynamic-update-slice_fusion.2
  99.1 2.6 bitcast_dynamic-update-slice_fusion.2
  102.4 2.7 bitcast_dynamic-update-slice_fusion.2
  105.7 2.7 bitcast_dynamic-update-slice_fusion.2
  109.1 2.7 bitcast_dynamic-update-slice_fusion.2
  112.4 2.7 bitcast_dynamic-update-slice_fusion.2
  115.7 2.5 multiply_convert_fusion.2
  118.2 10.7 %multiply_convert_fusion = bf16[32,256,256]{1,2,0:T(8,128)(2,1)S(1)} fusion(f32[256]{0:T(256)S(1)} %multiply_sqrt_fusion, bf16[32,1024,256]{2,1,0:T(8,128)(2,1)} %get-tuple-element.12, bf16[1024,128]{0,1:T(8,128)(2,1)S(1)} %get-tuple-element.22, bf16[1024,128]{0,1:T(8,128)(2,1)S(1)} %get-tuple-element.21), kind=kOutput, calls=%fused_computation.4 | convolution fusion | flops 4300210176 | bytes 21496832 | tf_op jit(solution)/shard_map/tk,btp->bkp/dot_general | solution.py:48
  134.2 115.3 %all_to_all.5 = bf16[64,32,2,2,256]{4,3,2,1,0:T(2,128)(2,1)S(1)} all-to-all(bf16[64,32,2,2,256]{4,3,2,1,0:T(2,128)(2,1)S(1)} %constant_dynamic-update-slice_fusion), channel_id=1, replica_groups=mesh['blk'=4,'pts'=64] {'pts'}, dimensions={0} | all-to-all | bytes 8388608 | tf_op jit(solution)/shard_map/all_to_all | solution.py:56
  249.5 4.4 copy.5
  253.8 7.4 %reshape.26 = bf16[32,2,2,16384]{3,0,2,1:T(8,128)(2,1)} reshape(bf16[32,2,2,64,256]{4,3,0,2,1:T(8,128)(2,1)} %copy.5) | data formatting | bytes 8388608 | tf_op jit(solution)/shard_map/reshape | solution.py:55
  261.2 285.5 %all-gather.2.cloned.1.call-done = bf16[128,2,2,16384]{3,0,2,1:T(8,128)(2,1)} async-done(((bf16[32,2,2,16384]{3,0,2,1:T(8,128)(2,1)}), bf16[128,2,2,16384]{3,0,2,1:T(8,128)(2,1)}) %all-gather.2.cloned.1.call-update) | async-done | bytes 16777232 | tf_op jit(solution)/shard_map/all_gather | solution.py:59
  546.7 7.1 %fusion = f32[2,32,128]{2,1,0:T(8,128)S(1)} fusion(bf16[128,2,2,16384]{3,0,2,1:T(8,128)(2,1)} %all-gather.2.cloned.1.call-done, bf16[32,2,2,16384]{3,0,2,1:T(8,128)(2,1)} %reshape.26), kind=kOutput, calls=%fused_computation.5 | convolution fusion | flops 268435456 | bytes 10518528 | tf_op jit(solution)/shard_map/bfp,nfp->fbn/dot_general | solution.py:31
  553.8 7.0 %fusion.1 = f32[2,32,128]{2,1,0:T(8,128)S(1)} fusion(bf16[128,2,2,16384]{3,0,2,1:T(8,128)(2,1)} %all-gather.2.cloned.1.call-done, bf16[32,2,2,16384]{3,0,2,1:T(8,128)(2,1)S(1)} %copy-done), kind=kOutput, calls=%fused_computation.6 | convolution fusion | flops 268435456 | bytes 10518528 | tf_op jit(solution)/shard_map/bfp,nfp->fbn/dot_general | solution.py:26
  560.9 2.9 fusion.7
  563.8 3.0 fusion.5
  566.8 0.6 copy.6
  (123 shorter events, 16.4 us)
Async XLA Ops:
  6.5 109.2 %copy-start.1 = (s32[128]{0:T(128)S(1)}, s32[128]{0:T(128)}, u32[]{:S(2)}) copy-start(s32[128]{0:T(128)} %param.6) | copy-start | bytes 1540
  6.5 540.2 %all-gather.2.cloned.1.call-start = ((), (), s32[]{:S(2)}) async-start(), calls=%async_computation.1 | async-start | bytes 20971520 | tf_op jit(solution)/shard_map/all_gather | solution.py:59
  546.7 7.1 %copy-start = (bf16[32,2,2,16384]{3,0,2,1:T(8,128)(2,1)S(1)}, bf16[32,2,2,16384]{3,0,2,1:T(8,128)(2,1)}, u32[]{:S(2)}) copy-start(bf16[32,2,2,16384]{3,0,2,1:T(8,128)(2,1)} %reshape.26) | copy-start | bytes 12582916
  546.7 14.1 %copy-start.2 = (bf16[128,2,2,16384]{3,0,2,1:T(8,128)(2,1)S(1)}, bf16[128,2,2,16384]{3,0,2,1:T(8,128)(2,1)}, u32[]{:S(2)}) copy-start(bf16[128,2,2,16384]{3,0,2,1:T(8,128)(2,1)} %all-gather.2.cloned.1.call-done) | copy-start | bytes 50331652
Sparse Core Ops, SparseCore 0:
  261.3 285.3 all-gather.1
